TPU v7x, 32 devices: a whole 2x2x4 slice. The times are simulated.
32 devices in a mesh: pole: 2 (over y), row: 8 (over z, x), col: 2 (over core).
Axes of the slice: x: 2, y: 2, z: 4, core: 2. Of those that a mesh axis runs over, the one named last changes fastest.
Arguments:
- known_inverse: float32 [16, 128, 1024], P('pole', 'col', 'row'), parts along dimension 0, may hold values from -1 to 3, as said below
- first_factor: float32 [2048, 512], P(('pole', 'row')), parts along dimension 0, may hold values from -0.5 to 0.5
- first_corner: float32 [1024, 512], P('pole'), parts along dimension 0, may hold values from -1 to 5, as said below
- first_ancestors: int32 [1024], P('pole'), parts along dimension 0, may hold values from 0 to 1023, as said below
- second_factor: float32 [2048, 512], P(('pole', 'row')), parts along dimension 0, may hold values from -0.75 to 0.75
- second_link: float32 [1024, 512], P('pole'), parts along dimension 0, may hold values from -0.25 to 0.25
- second_corner: float32 [1024, 512], P('pole', 'col'), parts along dimension 0, may hold values from -1 to 5, as said below
- second_ancestors: int32 [512], P('pole'), parts along dimension 0, may hold values from 0 to 1023, as said below
Outputs:
- first_column: float32 [2048, 512], P(('pole', 'row'), 'col'), parts along dimension 0
- first_diagonal: float32 [1024, 512], P('pole', 'col'), parts along dimension 0
- second_column: float32 [2048, 512], P(('pole', 'row'), 'col'), parts along dimension 0
- second_cross: float32 [1024, 512], P('pole', 'col'), parts along dimension 0
- second_diagonal: float32 [1024, 512], P('pole', 'col'), parts along dimension 0
There are 2 independent parts, one for each index of `pole`. A program takes and returns all parts, laid end to end along the dimension named above; each array names one. Nothing has to cross between parts.
Inputs may be any that keep to these rules, and one draw needn't show every extreme that they name: `known_inverse`: K is symmetric. `first_corner`: symmetric. `second_corner`: symmetric. `first_ancestors`: distinct row numbers; every block of 128 consecutive row numbers starting at a multiple of 128 holds at least one of them. `second_ancestors`: distinct row numbers, each of which is also in first_ancestors; every block of 128 consecutive row numbers starting at a multiple of 128 holds at least one of them.
All inputs are finite; a program needn't handle non-finite values.
Results may differ from a plain program's by a relative error of at most 0.000084.
Values sent between devices are 32-bit elements; how exact they have to be, the bound alone decides.
A program may use at most 128 MiB of HBM per device.

v0:
```python
import jax
import jax.numpy as jnp
from jax import lax
from jax.sharding import PartitionSpec as P

HIGH = lax.Precision.HIGHEST


def product(left, right):
    return jnp.dot(left, right, precision=HIGH, preferred_element_type=jnp.float32)


def transposed_product(left, right):
    return lax.dot_general(
        left, right, (((0,), (0,)), ((), ())), precision=HIGH, preferred_element_type=jnp.float32
    )


def local_mask(ancestors, row_start, block_rows):
    global_rows = row_start + jnp.arange(block_rows, dtype=jnp.int32)
    return jnp.any(ancestors[:, None] == global_rows[None, :], axis=0).astype(jnp.float32)[:, None]


def on_device(
    known_inverse,
    first_factor,
    first_corner,
    first_ancestors,
    second_factor,
    second_link,
    second_corner,
    second_ancestors,
):
    groups, share_rows, block_rows = known_inverse.shape
    half_width = second_corner.shape[1]
    col_index = lax.axis_index("col")
    row_start = lax.axis_index("row") * block_rows
    first_mask = local_mask(first_ancestors, row_start, block_rows)
    second_mask = local_mask(second_ancestors, row_start, block_rows)
    first_masked = first_factor * first_mask
    second_masked = second_factor * second_mask
    share_start = col_index * share_rows
    first_piece = lax.dynamic_slice_in_dim(first_masked, share_start, share_rows, 0)
    second_piece = lax.dynamic_slice_in_dim(second_masked, share_start, share_rows, 0)
    columns = known_inverse.reshape(groups * share_rows, block_rows)

    def add_piece(piece):
        return transposed_product(columns, piece)

    first_partial = add_piece(lax.all_gather(first_piece, "row", axis=0, tiled=True))
    second_partial = add_piece(lax.all_gather(second_piece, "row", axis=0, tiled=True))
    first_image = lax.psum_scatter(first_partial, "col", scatter_dimension=1, tiled=True)
    first_column = -(first_image * first_mask)
    first_full = lax.all_gather(first_column, "col", axis=1, tiled=True)
    diagonal_partial = transposed_product(first_masked, first_column)
    corner_half = lax.dynamic_slice_in_dim(first_corner, col_index * half_width, half_width, 1)
    first_diagonal = corner_half - lax.psum(diagonal_partial, "row")
    diagonal_full = lax.all_gather(first_diagonal, "col", axis=1, tiled=True)
    second_image = lax.psum_scatter(second_partial, "col", scatter_dimension=1, tiled=True)
    link_half = lax.dynamic_slice_in_dim(second_link, col_index * half_width, half_width, 1)
    second_column = -((second_image + product(first_full, link_half)) * second_mask)
    second_half = lax.dynamic_slice_in_dim(second_masked, col_index * half_width, half_width, 1)
    cross_partial = transposed_product(first_full, second_half)
    closing_partial = transposed_product(second_masked, second_column)
    cross_total, closing_total = lax.psum((cross_partial, closing_partial), "row")
    second_cross = -(cross_total + product(diagonal_full, link_half))
    second_diagonal = second_corner - closing_total - transposed_product(second_link, second_cross)
    return (first_column, first_diagonal, second_column, second_cross, second_diagonal)


def solution(mesh):
    return jax.shard_map(
        on_device,
        mesh=mesh,
        in_specs=(
            P("pole", "col", "row"),
            P(("pole", "row"), None),
            P("pole", None),
            P("pole"),
            P(("pole", "row"), None),
            P("pole", None),
            P("pole", "col"),
            P("pole"),
        ),
        out_specs=(
            P(("pole", "row"), "col"),
            P("pole", "col"),
            P(("pole", "row"), "col"),
            P("pole", "col"),
            P("pole", "col"),
        ),
        check_vma=False,
    )
```

profile of v0, /device:TPU:0, one launch (start us, length us, event | category | flops | bytes accessed | tf_op | source)
XLA Modules:
  0.0 233.3 jit_solution(5799603692559722448)
XLA Ops:
  7.2 0.0 copy-start
  7.2 0.0 all-gather.4.cloned.1.call-start
  7.2 0.0 copy-start.8
  7.3 0.7 copy-done.8
  8.0 0.1 compare_reduce_fusion
  8.2 1.0 broadcast_multiply_fusion.1
  9.2 0.0 copy-start.6
  9.2 0.7 constant_dynamic-slice_fusion.1
  9.9 0.0 copy-start.9
  9.9 0.0 all-gather.4.cloned.1.call-update
  9.9 0.0 all-gather.6.cloned.1.call-start
  10.0 0.6 copy-done.9
  10.6 0.1 compare_reduce_fusion.1
  10.7 0.0 copy-done.6
  10.7 0.1 broadcast_multiply_fusion
  10.8 0.0 copy-start.2
  10.8 0.7 constant_dynamic-slice_fusion
  11.5 0.0 all-gather.6.cloned.1.call-update
  11.5 0.0 reduce-scatter.3.cloned.1.call-start
  11.5 42.2 %all-gather.4.cloned.1.call-done = f32[512,512]{1,0:T(8,128)} async-done(((f32[64,512]{1,0:T(8,128)}), f32[512,512]{1,0:T(8,128)}) %all-gather.4.cloned.1.call-update) | async-done | bytes 1048592 | tf_op jit(solution)/shard_map/all_gather | solution.py:50
  53.7 0.0 copy-done.2
  53.7 3.7 %convolution_bitcast_fusion.2 = f32[128,512]{0,1:T(8,128)} fusion(f32[512,512]{1,0:T(8,128)} %all-gather.4.cloned.1.call-done, f32[512,128]{1,0:T(8,128)S(1)} %bitcast.22), kind=kOutput, calls=%fused_computation.5 | convolution fusion | flops 402653184 | bytes 1572864 | tf_op jit(solution)/shard_map/dot_general | solution.py:14
  57.5 0.0 reduce-scatter.3.cloned.1.call-update
  57.5 0.0 reduce-scatter.5.cloned.1.call-start
  57.5 37.9 %all-gather.6.cloned.1.call-done = f32[512,512]{1,0:T(8,128)} async-done(((f32[64,512]{1,0:T(8,128)}), f32[512,512]{1,0:T(8,128)}) %all-gather.6.cloned.1.call-update) | async-done | bytes 1048592 | tf_op jit(solution)/shard_map/all_gather | solution.py:51
  95.4 3.7 %convolution_bitcast_fusion.1 = f32[128,512]{0,1:T(8,128)} fusion(f32[512,512]{1,0:T(8,128)} %all-gather.6.cloned.1.call-done, f32[512,128]{1,0:T(8,128)S(1)} %bitcast.23), kind=kOutput, calls=%fused_computation.4 | convolution fusion | flops 402653184 | bytes 1572864 | tf_op jit(solution)/shard_map/dot_general | solution.py:14
  99.2 0.0 reduce-scatter.5.cloned.1.call-update
  99.2 0.0 all-reduce.3.cloned.1.call-start
  99.2 5.5 %reduce-scatter.3.cloned.1.call-done = f32[128,256]{0,1:T(8,128)} async-done(((f32[128,512]{0,1:T(8,128)}), f32[128,256]{0,1:T(8,128)}) %reduce-scatter.3.cloned.1.call-update) | async-done | bytes 131088 | tf_op jit(solution)/shard_map/reduce_scatter | solution.py:52
  104.7 0.9 multiply_negate_fusion
  105.6 2.0 all_gather.14
  107.6 1.4 fusion.6
  109.0 1.4 fusion.11
  110.4 5.9 %reduce-scatter.5.cloned.1.call-done = f32[128,256]{0,1:T(8,128)} async-done(((f32[128,512]{0,1:T(8,128)}), f32[128,256]{0,1:T(8,128)}) %reduce-scatter.5.cloned.1.call-update) | async-done | bytes 131088 | tf_op jit(solution)/shard_map/reduce_scatter | solution.py:59
  116.3 0.0 copy-done
  116.3 1.9 fusion.3
  118.2 0.0 copy-start.7
  118.2 1.4 fusion.12
  119.6 0.0 all-reduce.3.cloned.1.call-update
  119.6 0.0 all-gather.8.cloned.1.call-start
  119.7 91.4 %all-reduce.3.cloned.1.call-done = (f32[512,256]{1,0:T(8,128)}, f32[512,256]{1,0:T(8,128)}, f32[512,256]{1,0:T(8,128)}) async-done(((f32[512,256]{1,0:T(8,128)}, f32[512,256]{1,0:T(8,128)}, f32[512,256]{1,0:T(8,128)}), (f32[512,256]{1,0:T(8,128)}, f32[512,256]{1,0:T(8,128)}, f32[512,256]{1,0:T(8,128)})) %all-reduce.3.cloned.1.call-update) | async-done | bytes 1572880 | tf_op jit(solution)/shard_map/psum | solution.py:57
  211.1 0.0 copy-done.7
  211.1 1.9 dynamic-slice_subtract_fusion
  213.0 0.0 copy-start.5
  213.1 0.0 all-gather.8.cloned.1.call-update
  213.1 0.8 copy.19
  213.8 0.8 copy.20
  214.6 6.9 %all-gather.8.cloned.1.call-done = f32[512,512]{1,0:T(8,128)} async-done(((f32[512,256]{1,0:T(8,128)}), f32[512,512]{1,0:T(8,128)}) %all-gather.8.cloned.1.call-update) | async-done | bytes 1048592 | tf_op jit(solution)/shard_map/all_gather | solution.py:58
  221.5 0.0 copy-done.5
  221.5 0.0 copy-start.3
  221.5 0.0 copy-start.4
  221.5 2.3 fusion
  223.8 0.0 copy-start.1
  223.8 0.0 copy-done.3
  223.8 0.0 copy-done.4
  223.8 2.6 %fusion.1 = f32[512,256]{1,0:T(8,128)} fusion(f32[512,256]{1,0:T(8,128)S(1)} %fusion, f32[512,512]{1,0:T(8,128)S(1)} %copy-done, f32[512,256]{1,0:T(8,128)S(1)} %copy-done.3, f32[512,256]{1,0:T(8,128)S(1)} %copy-done.4), kind=kOutput, calls=%fused_computation.3 | convolution fusion | flops 805568512 | bytes 3145728 | tf_op jit(solution)/shard_map/dot_general | solution.py:14
  226.4 0.0 copy-done.1
  (3 shorter events, 0.0 us)
Async XLA Ops:
  7.2 109.1 %copy-start = (f32[512,512]{1,0:T(8,128)S(1)}, f32[512,512]{1,0:T(8,128)}, u32[]{:S(2)}) copy-start(f32[512,512]{1,0:T(8,128)} %param.13) | copy-start | bytes 3145732
  7.2 46.5 %all-gather.4.cloned.1.call-start = ((), (), s32[]{:S(2)}) async-start(), calls=%async_computation.2 | async-start | bytes 1179648 | tf_op jit(solution)/shard_map/all_gather | solution.py:50
  7.2 0.8 copy-start.8
  9.2 1.5 copy-start.6
  9.9 0.7 copy-start.9
  9.9 85.5 %all-gather.6.cloned.1.call-start = ((), (), s32[]{:S(2)}) async-start(), calls=%async_computation.4 | async-start | bytes 1179648 | tf_op jit(solution)/shard_map/all_gather | solution.py:51
  10.8 42.9 %copy-start.2 = (f32[8,64,128]{2,1,0:T(8,128)S(1)}, f32[8,64,128]{2,1,0:T(8,128)}, u32[]{:S(2)}) copy-start(f32[8,64,128]{2,1,0:T(8,128)} %param.8) | copy-start | bytes 786436
  11.5 93.2 %reduce-scatter.3.cloned.1.call-start = ((), (), s32[]{:S(2)}) async-start(), calls=%async_computation.3 | async-start | bytes 393216 | tf_op jit(solution)/shard_map/reduce_scatter | solution.py:52
  57.5 58.8 %reduce-scatter.5.cloned.1.call-start = ((), (), s32[]{:S(2)}) async-start(), calls=%async_computation.5 | async-start | bytes 393216 | tf_op jit(solution)/shard_map/reduce_scatter | solution.py:59
  99.2 111.9 %all-reduce.3.cloned.1.call-start = ((), (), s32[]{:S(2)}) async-start(), calls=%async_computation.7 | async-start | bytes 3145728 | tf_op jit(solution)/shard_map/psum | solution.py:57
  118.2 93.0 %copy-start.7 = (f32[512,512]{1,0:T(8,128)S(1)}, f32[512,512]{1,0:T(8,128)}, u32[]{:S(2)}) copy-start(f32[512,512]{1,0:T(8,128)} %param.10) | copy-start | bytes 3145732
  119.6 101.8 %all-gather.8.cloned.1.call-start = ((), (), s32[]{:S(2)}) async-start(), calls=%async_computation.6 | async-start | bytes 1572864 | tf_op jit(solution)/shard_map/all_gather | solution.py:58
  213.0 8.4 %copy-start.5 = (f32[512,256]{1,0:T(8,128)S(1)}, f32[512,256]{1,0:T(8,128)}, u32[]{:S(2)}) copy-start(f32[512,256]{1,0:T(8,128)} %get-tuple-element.16) | copy-start | bytes 1572868
  221.5 2.3 copy-start.3
  221.5 2.3 copy-start.4
  223.8 2.7 %copy-start.1 = (f32[512,256]{1,0:T(8,128)}, f32[512,256]{1,0:T(8,128)S(1)}, u32[]{:S(2)}) copy-start(f32[512,256]{1,0:T(8,128)S(1)} %fusion) | copy-start | bytes 1572868
Sparse Core Ops, SparseCore 0:
  10.7 42.9 all-gather.3
  56.4 38.9 all-gather.5
  98.2 6.4 reduce-scatter.2
  107.4 8.8 reduce-scatter.4
  120.6 90.5 all-reduce.2
  213.2 8.2 all-gather.7
where the time goes:
time: 234 us; the launch traced here: 233 us
  waiting for transfers between devices  190 us (81%)
  matrix products  18.5 us (8%)
  between operations  14.2 us (6%)
  local copies, waits for them, and re-layouts  4.25 us (2%)
  other arithmetic  4.23 us (2%)
    psum x1, waiting for transfers between devices, on_device(): first_diagonal = corner_half - lax.psum(diagonal_partial, 'row')  91.4 us
    all_gather x1, waiting for transfers between devices, on_device(): lax.all_gather(first_piece, 'row', axis=0, tiled=True)  42.2 us
    all_gather x1, waiting for transfers between devices, on_device(): lax.all_gather(second_piece, 'row', axis=0, tiled=True)  37.9 us
    dot_general x6, matrix products, transposed_product(): lax.dot_general(left, right, (((0,), (0,)), ((), ())), precision=HIGH, pr...  14.3 us
    all_gather x1, waiting for transfers between devices, on_device(): diagonal_full = lax.all_gather(first_diagonal, 'col', axis=1, tiled=True)  6.88 us
    reduce_scatter x1, waiting for transfers between devices, on_device(): lax.psum_scatter(second_partial, 'col', scatter_dimension=1, tiled=True)  5.86 us
    reduce_scatter x1, waiting for transfers between devices, on_device(): lax.psum_scatter(first_partial, 'col', scatter_dimension=1, tiled=True)  5.48 us
  transfers between devices with their start and end apart: 6, of which 6 were waited for; matrix products, arithmetic and copies ran while one was open for 6% of the time, Pallas kernels for 0%

commit v1 on v0

--- a/solution.py
+++ b/solution.py
@@ -54,7 +54,8 @@
     first_full = lax.all_gather(first_column, "col", axis=1, tiled=True)
     diagonal_partial = transposed_product(first_masked, first_column)
     corner_half = lax.dynamic_slice_in_dim(first_corner, col_index * half_width, half_width, 1)
-    first_diagonal = corner_half - lax.psum(diagonal_partial, "row")
+    _handle_axis_part = lambda point: lax.all_gather(point, "row").sum(axis=0)
+    first_diagonal = corner_half - _handle_axis_part(diagonal_partial)
     diagonal_full = lax.all_gather(first_diagonal, "col", axis=1, tiled=True)
     second_image = lax.psum_scatter(second_partial, "col", scatter_dimension=1, tiled=True)
     link_half = lax.dynamic_slice_in_dim(second_link, col_index * half_width, half_width, 1)

time: 234 us -> 298 us (1.27)
  waiting for transfers between devices: 190 us -> 249 us
  other arithmetic: 4.23 us -> 9.18 us
    all_gather x0 -> x1, waiting for transfers between devices: none -> 71.7 us  [on_device(): _handle_axis_part = lambda point: lax.all_gather(point, 'row').sum(axis=0)]
    psum x1, waiting for transfers between devices: 91.4 us -> 74.8 us  [on_device(): lax.psum((cross_partial, closing_partial), 'row')]
    all_gather x1, waiting for transfers between devices: 6.88 us -> 10.8 us  [on_device(): diagonal_full = lax.all_gather(first_diagonal, 'col', axis=1, tiled=True)]
  transfers between devices with their start and end apart: 6 -> 7, of which waited for: 6 -> 7; matrix products, arithmetic and copies ran while one was open for 6% -> 8% of each run, Pallas kernels for 0% -> 0%
where the time goes in v1:
time: 298 us; the launch traced here: 297 us
  waiting for transfers between devices  249 us (84%)
  matrix products  19.9 us (7%)
  between operations  14.2 us (5%)
  other arithmetic  9.18 us (3%)
    psum x1, waiting for transfers between devices, on_device(): lax.psum((cross_partial, closing_partial), 'row')  74.8 us
    all_gather x1, waiting for transfers between devices, on_device(): _handle_axis_part = lambda point: lax.all_gather(point, 'row').sum(axis=0)  71.7 us
    all_gather x1, waiting for transfers between devices, on_device(): lax.all_gather(first_piece, 'row', axis=0, tiled=True)  41.2 us
    all_gather x1, waiting for transfers between devices, on_device(): lax.all_gather(second_piece, 'row', axis=0, tiled=True)  37.9 us
    dot_general x6, matrix products, transposed_product(): lax.dot_general(left, right, (((0,), (0,)), ((), ())), precision=HIGH, pr...  15.6 us
    all_gather x1, waiting for transfers between devices, on_device(): diagonal_full = lax.all_gather(first_diagonal, 'col', axis=1, tiled=True)  10.8 us
    reduce_scatter x1, waiting for transfers between devices, on_device(): lax.psum_scatter(second_partial, 'col', scatter_dimension=1, tiled=True)  7.14 us
  transfers between devices with their start and end apart: 7, of which 7 were waited for; matrix products, arithmetic and copies ran while one was open for 8% of the time, Pallas kernels for 0%

profile of v1, /device:TPU:0, one launch (start us, length us, event | category | flops | bytes accessed | tf_op | source)
XLA Modules:
  0.0 297.4 jit_solution(5994508977713043666)
XLA Ops:
  7.2 0.0 copy-start
  7.2 0.0 all-gather.6.cloned.1.call-start
  7.2 0.9 compare_reduce_fusion
  8.2 1.0 broadcast_multiply_fusion.1
  9.2 0.7 constant_dynamic-slice_fusion.1
  9.9 0.0 all-gather.6.cloned.1.call-update
  9.9 0.0 all-gather.8.cloned.1.call-start
  9.9 0.8 compare_reduce_fusion.1
  10.8 1.0 broadcast_multiply_fusion
  11.8 0.7 constant_dynamic-slice_fusion
  12.5 0.0 all-gather.8.cloned.1.call-update
  12.5 0.0 reduce-scatter.3.cloned.1.call-start
  12.5 41.2 %all-gather.6.cloned.1.call-done = f32[512,512]{1,0:T(8,128)} async-done(((f32[64,512]{1,0:T(8,128)}), f32[512,512]{1,0:T(8,128)}) %all-gather.6.cloned.1.call-update) | async-done | bytes 1048592 | tf_op jit(solution)/shard_map/all_gather | solution.py:50
  53.7 3.8 %convolution_bitcast_fusion.2 = f32[128,512]{0,1:T(8,128)} fusion(f32[512,512]{1,0:T(8,128)} %all-gather.6.cloned.1.call-done, f32[512,128]{1,0:T(8,128)} %bitcast.24), kind=kOutput, calls=%fused_computation.5 | convolution fusion | flops 402653184 | bytes 1572864 | tf_op jit(solution)/shard_map/dot_general | solution.py:14
  57.5 0.0 reduce-scatter.3.cloned.1.call-update
  57.5 0.0 reduce-scatter.5.cloned.1.call-start
  57.6 37.9 %all-gather.8.cloned.1.call-done = f32[512,512]{1,0:T(8,128)} async-done(((f32[64,512]{1,0:T(8,128)}), f32[512,512]{1,0:T(8,128)}) %all-gather.8.cloned.1.call-update) | async-done | bytes 1048592 | tf_op jit(solution)/shard_map/all_gather | solution.py:51
  95.4 3.8 %convolution_bitcast_fusion.1 = f32[128,512]{0,1:T(8,128)} fusion(f32[512,512]{1,0:T(8,128)} %all-gather.8.cloned.1.call-done, f32[512,128]{1,0:T(8,128)} %bitcast.25), kind=kOutput, calls=%fused_computation.4 | convolution fusion | flops 402653184 | bytes 1572864 | tf_op jit(solution)/shard_map/dot_general | solution.py:14
  99.2 0.0 reduce-scatter.5.cloned.1.call-update
  99.2 0.0 all-gather.12.cloned.1.call-start
  99.3 5.4 %reduce-scatter.3.cloned.1.call-done = f32[128,256]{0,1:T(8,128)} async-done(((f32[128,512]{0,1:T(8,128)}), f32[128,256]{0,1:T(8,128)}) %reduce-scatter.3.cloned.1.call-update) | async-done | bytes 131088 | tf_op jit(solution)/shard_map/reduce_scatter | solution.py:52
  104.7 0.9 multiply_negate_fusion
  105.6 1.4 fusion.11
  107.1 0.0 all-gather.12.cloned.1.call-update
  107.1 0.0 all-reduce.3.cloned.1.call-start
  107.1 2.0 all_gather.22
  109.1 7.1 %reduce-scatter.5.cloned.1.call-done = f32[128,256]{0,1:T(8,128)} async-done(((f32[128,512]{0,1:T(8,128)}), f32[128,256]{0,1:T(8,128)}) %reduce-scatter.5.cloned.1.call-update) | async-done | bytes 131088 | tf_op jit(solution)/shard_map/reduce_scatter | solution.py:60
  116.3 0.0 copy-done
  116.3 1.9 fusion.3
  118.2 1.4 fusion.6
  119.5 1.4 fusion.12
  121.0 0.0 all-reduce.3.cloned.1.call-update
  121.0 0.0 all-gather.10.cloned.1.call-start
  121.1 71.7 %all-gather.12.cloned.1.call-done = f32[4096,256]{1,0:T(8,128)} async-done(((f32[512,256]{1,0:T(8,128)}), f32[4096,256]{1,0:T(8,128)}) %all-gather.12.cloned.1.call-update) | async-done | bytes 4194320 | tf_op jit(solution)/shard_map/all_gather | solution.py:57
  192.8 0.0 copy-start.2
  192.8 2.6 reduce_sum.9
  195.3 1.9 dynamic-slice_subtract_fusion
  197.2 0.0 all-gather.10.cloned.1.call-update
  197.3 0.8 copy.19
  198.0 0.8 copy.20
  198.8 74.8 %all-reduce.3.cloned.1.call-done = (f32[512,256]{1,0:T(8,128)}, f32[512,256]{1,0:T(8,128)}) async-done(((f32[512,256]{1,0:T(8,128)}, f32[512,256]{1,0:T(8,128)}), (f32[512,256]{1,0:T(8,128)}, f32[512,256]{1,0:T(8,128)})) %all-reduce.3.cloned.1.call-update) | async-done | bytes 1048592 | tf_op jit(solution)/shard_map/psum | solution.py:66
  273.6 10.8 %all-gather.10.cloned.1.call-done = f32[512,512]{1,0:T(8,128)} async-done(((f32[512,256]{1,0:T(8,128)}), f32[512,512]{1,0:T(8,128)}) %all-gather.10.cloned.1.call-update) | async-done | bytes 1048592 | tf_op jit(solution)/shard_map/all_gather | solution.py:59
  284.4 2.3 fusion
  286.7 0.0 copy-start.1
  286.7 0.0 copy-done.2
  286.7 3.8 %fusion.1 = f32[512,256]{1,0:T(8,128)} fusion(f32[512,256]{1,0:T(8,128)S(1)} %fusion, f32[512,512]{1,0:T(8,128)S(1)} %copy-done, f32[512,256]{1,0:T(8,128)S(1)} %copy-done.2, f32[512,256]{1,0:T(8,128)} %get-tuple-element.16), kind=kOutput, calls=%fused_computation.3 | convolution fusion | flops 805568512 | bytes 3145728 | tf_op jit(solution)/shard_map/dot_general | solution.py:14
  290.6 0.0 copy-done.1
  (3 shorter events, 0.0 us)
Async XLA Ops:
  7.2 109.1 %copy-start = (f32[512,512]{1,0:T(8,128)S(1)}, f32[512,512]{1,0:T(8,128)}, u32[]{:S(2)}) copy-start(f32[512,512]{1,0:T(8,128)} %param.13) | copy-start | bytes 3145732
  7.2 46.5 %all-gather.6.cloned.1.call-start = ((), (), s32[]{:S(2)}) async-start(), calls=%async_computation.2 | async-start | bytes 1179648 | tf_op jit(solution)/shard_map/all_gather | solution.py:50
  9.9 85.5 %all-gather.8.cloned.1.call-start = ((), (), s32[]{:S(2)}) async-start(), calls=%async_computation.4 | async-start | bytes 1179648 | tf_op jit(solution)/shard_map/all_gather | solution.py:51
  12.5 92.2 %reduce-scatter.3.cloned.1.call-start = ((), (), s32[]{:S(2)}) async-start(), calls=%async_computation.3 | async-start | bytes 393216 | tf_op jit(solution)/shard_map/reduce_scatter | solution.py:52
  57.5 58.8 %reduce-scatter.5.cloned.1.call-start = ((), (), s32[]{:S(2)}) async-start(), calls=%async_computation.5 | async-start | bytes 393216 | tf_op jit(solution)/shard_map/reduce_scatter | solution.py:60
  99.2 93.5 %all-gather.12.cloned.1.call-start = ((), (), s32[]{:S(2)}) async-start(), calls=%async_computation.7 | async-start | bytes 4718592 | tf_op jit(solution)/shard_map/all_gather | solution.py:57
  107.1 166.5 %all-reduce.3.cloned.1.call-start = ((), (), s32[]{:S(2)}) async-start(), calls=%async_computation.8 | async-start | bytes 2097152 | tf_op jit(solution)/shard_map/psum | solution.py:66
  121.0 163.4 %all-gather.10.cloned.1.call-start = ((), (), s32[]{:S(2)}) async-start(), calls=%async_computation.6 | async-start | bytes 1572864 | tf_op jit(solution)/shard_map/all_gather | solution.py:59
  192.8 94.0 %copy-start.2 = (f32[512,256]{1,0:T(8,128)S(1)}, f32[512,256]{1,0:T(8,128)}, u32[]{:S(2)}) copy-start(f32[512,256]{1,0:T(8,128)} %param.14) | copy-start | bytes 1572868
  286.7 3.9 %copy-start.1 = (f32[512,256]{1,0:T(8,128)}, f32[512,256]{1,0:T(8,128)S(1)}, u32[]{:S(2)}) copy-start(f32[512,256]{1,0:T(8,128)S(1)} %fusion) | copy-start | bytes 1572868
Sparse Core Ops, SparseCore 0:
  10.7 42.9 all-gather.5
  56.4 38.9 all-gather.7
  98.2 6.4 reduce-scatter.2
  107.4 8.8 reduce-scatter.4
  118.8 73.8 all-gather.11
  196.7 76.7 all-reduce.2
  275.7 8.6 all-gather.9
